TPU v7x, 256 devices: a whole 4x4x8 slice. The times are simulated.
256 devices in a mesh: seq: 32 (over z, x_lo, core), fsdp: 8 (over x_hi, y).
Axes of the slice: x: 4 (x_hi: 2, x_lo: 2; x = x_hi * 2 + x_lo), y: 4, z: 8, core: 2. Of those that a mesh axis runs over, the one named last changes fastest.
Arguments:
- hidden_next: bfloat16 [8192, 8192], P('seq'), may hold values from -6 to 6
- values_next: bfloat16 [8192, 8192], P('seq', 'fsdp'), may hold values from -6 to 6
- seg_next: int32 [4], replicated, may hold values from 1 to 4096, 8192 in all
- proj_bc: bfloat16 [8192, 1024], P(('seq', 'fsdp')), may hold values from -0.09375 to 0.09375
- proj_dt: bfloat16 [8192, 128], P(('seq', 'fsdp')), may hold values from -0.0625 to 0.0625
- dt_bias: float32 [128], replicated, may hold values from -4 to -2.5
- decay_rate: float32 [128], replicated, may hold values from 0 to 1, as said below
- skip_gain: float32 [128], replicated, may hold values from 0.5 to 1.5
- bc_prev: bfloat16 [8192, 1024], P('seq'), may hold values from -4 to 4
- dt_prev: float32 [8192, 128], P('seq', 'fsdp'), may hold values from 0.01 to 0.3
- seg_prev: int32 [4], replicated, may hold values from 1 to 4096, 8192 in all
- grad_prev: bfloat16 [8192, 8192], P('seq', 'fsdp'), may hold values from -6 to 6
Outputs:
- out_next: bfloat16 [8192, 8192], P('seq', 'fsdp')
- grad_values: bfloat16 [8192, 8192], P('seq', 'fsdp')
Inputs may be any that keep to these rules, and one draw needn't show every extreme that they name: `seg_next`: lengths of the rollout's 4 segments in order, summing to 8192. `seg_prev`: lengths of the rollout's 4 segments in order, summing to 8192. `decay_rate`: positive.
All inputs are finite; a program needn't handle non-finite values.
Results may differ from a plain program's by a relative error of at most 0.0064.
Values may be sent and summed in bfloat16 or wider, within the bound.
A program may use at most 128 MiB of HBM per device.

v0:
```python
import functools

import jax
import jax.numpy as jnp
from jax import lax
from jax.experimental import pallas as pl
from jax.experimental.pallas import tpu as pltpu
from jax.sharding import PartitionSpec as P

GW = 4
SPAN = 128
LANES = 128
MESH = pl.DeviceIdType.MESH


def scan_kernel(
    back, count, nblocks, heads, groups, head_dim,
    len_ref, x_ref, p_ref, q_ref, dt_ref, decay_ref, skip_ref,
    out_ref,
    cum_s, cum_t, dt_t, fin_s, fout_s, fexp, inside, pre, keep, inbox, outbox, send_sem, recv_sem,
):
    me = lax.axis_index("seq")
    place = count - 1 - me if back else me
    nxt = me - 1 if back else me + 1
    prv = me + 1 if back else me - 1
    npair = heads * head_dim // LANES
    per = LANES // head_dim
    pair_group = npair // groups
    first, last = place == 0, place == count - 1

    barrier = pltpu.get_barrier_semaphore()

    @pl.when(jnp.logical_not(first))
    def _():
        pl.semaphore_signal(barrier, inc=1, device_id={"seq": prv}, device_id_type=MESH)

    @pl.when(jnp.logical_not(last))
    def _():
        pl.semaphore_signal(barrier, inc=1, device_id={"seq": nxt}, device_id_type=MESH)

    bound = []
    total = jnp.int32(0)
    for k in range(3):
        total = total + len_ref[k]
        bound.append(total)

    def seg_of(pos):
        s = jnp.zeros_like(pos)
        for b in bound:
            s = s + (b <= pos).astype(jnp.int32)
        return s

    slab = me * (nblocks * SPAN)
    dim0 = lax.broadcasted_iota(jnp.int32, (SPAN, SPAN), 0)
    dim1 = lax.broadcasted_iota(jnp.int32, (SPAN, SPAN), 1)
    lane = lax.broadcasted_iota(jnp.int32, (1, LANES), 1)
    tril = (dim0 >= dim1).astype(jnp.float32)

    def widen(a, c):
        res = a[:, c * per:c * per + 1]
        for k in range(1, per):
            res = jnp.where(lane >= k * head_dim, a[:, c * per + k:c * per + k + 1], res)
        return jnp.broadcast_to(res, (a.shape[0], LANES))

    for c in range(npair):
        pre[0, c] = jnp.zeros((LANES, LANES), jnp.float32)
        keep[0, c] = jnp.ones((1, LANES), jnp.float32)

    for step in range(nblocks):
        b = nblocks - 1 - step if back else step
        rows = slice(b * SPAN, (b + 1) * SPAN)
        dt = dt_ref[rows, :]
        cum = jnp.dot(tril, -(dt * decay_ref[...]), precision=lax.Precision.HIGHEST,
                      preferred_element_type=jnp.float32)
        end = cum[SPAN - 1:SPAN, :]
        cum_s[rows, :] = cum
        cum_t[b] = cum.T
        dt_t[b] = dt.T
        pos = slab + b * SPAN + lax.broadcasted_iota(jnp.int32, (SPAN, heads), 0)
        seg = seg_of(pos)
        edge = slab + b * SPAN + lax.broadcasted_iota(jnp.int32, (1, heads), 0) * 0
        seg_e = seg_of(edge + (SPAN - 1))
        seg_b = jnp.where(edge == 0, 0, seg_of(edge - 1))
        send = jnp.where(seg == seg_e, jnp.exp(end - cum), 0.0)
        read = jnp.where(seg == seg_b, jnp.exp(cum), 0.0)
        carry = jnp.where(seg_e == seg_b, jnp.exp(end), 0.0)
        f_in = read if back else send * dt
        fin_s[rows, :] = f_in
        fout_s[rows, :] = send * dt if back else read
        qt = [q_ref[rows, g * LANES:(g + 1) * LANES].T for g in range(groups)]
        for c in range(npair):
            cols = slice(c * LANES, (c + 1) * LANES)
            sent = (x_ref[rows, cols].astype(jnp.float32) * widen(f_in, c)).astype(jnp.bfloat16)
            loc = jnp.dot(qt[c // pair_group], sent, preferred_element_type=jnp.float32)
            wide = widen(carry, c)
            pre[step + 1, c] = wide * pre[step, c] + loc
            keep[step + 1, c] = wide * keep[step, c]

    def in_block():
        def one(b, _):
            start = pl.multiple_of(b * SPAN, SPAN)
            rows = pl.ds(start, SPAN)
            seg_i = seg_of(slab + start + dim0)
            seg_j = seg_of(slab + start + dim1)
            order = (dim1 >= dim0) if back else (dim1 <= dim0)
            bias = jnp.where((seg_i == seg_j) & order, 0.0, -jnp.inf)
            cum = cum_s[rows, :]
            dt = dt_ref[rows, :]
            f_out = fout_s[rows, :]
            for g in range(groups):
                gl = slice(g * LANES, (g + 1) * LANES)
                score = lax.dot_general(p_ref[rows, gl], q_ref[rows, gl], (((1,), (1,)), ((), ())),
                                        preferred_element_type=jnp.float32)
                for c in range(g * pair_group, (g + 1) * pair_group):
                    cols = slice(c * LANES, (c + 1) * LANES)
                    x = x_ref[rows, cols]
                    mixes, parts = [], []
                    for k in range(per):
                        h = c * per + k
                        col = cum[:, h:h + 1]
                        row = cum_t[b, h:h + 1, :]
                        spread = (row - col) if back else (col - row)
                        w = jnp.exp(spread + bias) * score
                        if not back:
                            w = w * dt_t[b, h:h + 1, :]
                        mixes.append(w.astype(jnp.bfloat16))
                        mine = (lane >= k * head_dim) & (lane < (k + 1) * head_dim)
                        parts.append(jnp.where(mine, x, jnp.zeros_like(x)))
                    acc = jnp.dot(jnp.concatenate(mixes, 1), jnp.concatenate(parts, 0),
                                  preferred_element_type=jnp.float32)
                    if back:
                        acc = acc * widen(dt, c)
                    inside[c, rows, :] = acc + widen(skip_ref[...], c) * x.astype(jnp.float32)
                    fexp[c, rows, :] = widen(f_out, c)
            return 0

        lax.fori_loop(0, nblocks, one, 0)

    def finish(c, state):
        g = c // pair_group
        cols = pl.ds(pl.multiple_of(c * LANES, LANES), LANES)
        gl = pl.ds(pl.multiple_of(g * LANES, LANES), LANES)
        for step in range(nblocks):
            b = nblocks - 1 - step if back else step
            rows = slice(b * SPAN, (b + 1) * SPAN)
            entering = (keep[step, c] * state + pre[step, c]).astype(jnp.bfloat16)
            y = jnp.dot(p_ref[rows, gl], entering, preferred_element_type=jnp.float32)
            out_ref[rows, cols] = (inside[c, rows, :] + fexp[c, rows, :] * y).astype(jnp.bfloat16)

    def hop(c):
        return pltpu.make_async_remote_copy(
            src_ref=outbox.at[c], dst_ref=inbox.at[c], send_sem=send_sem.at[c],
            recv_sem=recv_sem.at[c], device_id={"seq": nxt}, device_id_type=MESH)

    late = place >= 5

    @pl.when(first)
    def _():
        inbox[...] = jnp.zeros_like(inbox)

    pl.semaphore_wait(barrier, jnp.where(first, 0, 1) + jnp.where(last, 0, 1))

    def relay(c, _):
        @pl.when(jnp.logical_not(first))
        def _():
            hop(c).wait_recv()

        state = inbox[c].astype(jnp.float32)

        @pl.when(jnp.logical_not(last))
        def _():
            outbox[c] = (keep[nblocks, c] * state + pre[nblocks, c]).astype(jnp.bfloat16)
            hop(c).start()

        @pl.when(late)
        def _():
            finish(c, state)

        return 0

    def phase(ph, _):
        @pl.when(ph == jnp.where(late, 0, 1))
        def _():
            in_block()

        @pl.when(ph == 0)
        def _():
            lax.fori_loop(0, npair, relay, 0)

        return 0

    lax.fori_loop(0, 2, phase, 0)

    @pl.when(jnp.logical_not(late))
    def _():
        def one(c, _):
            finish(c, inbox[c].astype(jnp.float32))
            return 0

        lax.fori_loop(0, npair, one, 0)

    @pl.when(jnp.logical_not(last))
    def _():
        def one(c, _):
            hop(c).wait_send()
            return 0

        lax.fori_loop(0, npair, one, 0)


def scan_pass(back, lengths, x, p_vec, q_vec, dt, decay, skip):
    tokens, width = x.shape
    heads = dt.shape[1]
    groups = p_vec.shape[1] // LANES
    head_dim = width // heads
    nblocks = tokens // SPAN
    npair = width // LANES
    count = lax.axis_size("seq")
    vm = pl.BlockSpec(memory_space=pltpu.VMEM)
    f32, bf16 = jnp.float32, jnp.bfloat16
    return pl.pallas_call(
        functools.partial(scan_kernel, back, count, nblocks, heads, groups, head_dim),
        out_shape=jax.ShapeDtypeStruct((tokens, width), bf16),
        in_specs=[pl.BlockSpec(memory_space=pltpu.SMEM)] + [vm] * 6,
        out_specs=vm,
        scratch_shapes=[
            pltpu.VMEM((tokens, heads), f32),
            pltpu.VMEM((nblocks, heads, SPAN), f32),
            pltpu.VMEM((nblocks, heads, SPAN), f32),
            pltpu.VMEM((tokens, heads), f32),
            pltpu.VMEM((tokens, heads), f32),
            pltpu.VMEM((npair, tokens, LANES), f32),
            pltpu.VMEM((npair, tokens, LANES), f32),
            pltpu.VMEM((nblocks + 1, npair, LANES, LANES), f32),
            pltpu.VMEM((nblocks + 1, npair, 1, LANES), f32),
            pltpu.VMEM((npair, LANES, LANES), bf16),
            pltpu.VMEM((npair, LANES, LANES), bf16),
            pltpu.SemaphoreType.DMA((npair,)),
            pltpu.SemaphoreType.DMA((npair,)),
        ],
        compiler_params=pltpu.CompilerParams(
            collective_id=1 if back else 0, has_side_effects=True,
            vmem_limit_bytes=40 * 1024 * 1024),
        cost_estimate=pl.CostEstimate(
            flops=40_000_000_000, bytes_accessed=8 * tokens * width, transcendentals=0),
        name="back_pass" if back else "next_pass",
    )(lengths, x, p_vec, q_vec, dt, decay, skip)


def body(
    hidden_next, values_next, seg_next, proj_bc, proj_dt, dt_bias, decay_rate, skip_gain,
    bc_prev, dt_prev, seg_prev, grad_prev,
):
    tokens_dev = hidden_next.shape[0]
    bc_width = proj_bc.shape[1]
    heads_all = proj_dt.shape[1]
    fsdp_count = lax.axis_size("fsdp")
    fsdp_place = lax.axis_index("fsdp")
    seq_count = lax.axis_size("seq")
    heads_dev = heads_all // fsdp_count
    state_dim = bc_width // (2 * GW)
    per_group = heads_all // GW
    groups_dev = max(1, heads_dev // per_group)
    first_head = fsdp_place * heads_dev
    first_group = first_head // per_group
    rows_dev = proj_bc.shape[0]
    half = bc_width // 2
    gw = groups_dev * state_dim

    pieces = []
    for f in range(fsdp_count):
        g0 = (f * heads_dev // per_group) * state_dim
        pieces += [proj_bc[:, g0:g0 + gw], proj_bc[:, half + g0:half + g0 + gw],
                   proj_dt[:, f * heads_dev:(f + 1) * heads_dev]]
    cols = 2 * gw + heads_dev
    weights = lax.all_gather(jnp.concatenate(pieces, axis=1), "seq", axis=0, tiled=True)

    decay = lax.dynamic_slice_in_dim(decay_rate, first_head, heads_dev, 0)[None]
    skip = lax.dynamic_slice_in_dim(skip_gain, first_head, heads_dev, 0)[None]
    bias = lax.dynamic_slice_in_dim(dt_bias, first_head, heads_dev, 0)[None]

    b_prev = lax.dynamic_slice_in_dim(bc_prev, first_group * state_dim, gw, 1)
    c_prev = lax.dynamic_slice_in_dim(bc_prev, half + first_group * state_dim, gw, 1)
    grad_values = scan_pass(True, seg_prev, grad_prev, b_prev, c_prev, dt_prev, decay, skip)

    owned = lax.dynamic_slice_in_dim(
        hidden_next.reshape(tokens_dev, seq_count, fsdp_count, rows_dev), fsdp_place, 1, 2
    ).reshape(tokens_dev, seq_count * rows_dev)
    owned, grad_values = lax.optimization_barrier((owned, grad_values))
    if fsdp_count == 2:
        other = lax.dynamic_slice_in_dim(weights, (1 - fsdp_place) * cols, cols, 1)
        mine = lax.dynamic_slice_in_dim(weights, fsdp_place * cols, cols, 1)
        away = lax.ppermute(jnp.dot(owned, other, preferred_element_type=jnp.float32),
                            "fsdp", [(0, 1), (1, 0)])
        sums = jnp.dot(owned, mine, preferred_element_type=jnp.float32) + away
    else:
        sums = lax.psum_scatter(jnp.dot(owned, weights, preferred_element_type=jnp.float32),
                                "fsdp", scatter_dimension=1, tiled=True)
    b_next = sums[:, :gw].astype(jnp.bfloat16)
    c_next = sums[:, gw:2 * gw].astype(jnp.bfloat16)
    dt_next = jax.nn.softplus(sums[:, 2 * gw:] + bias)
    out_next = scan_pass(False, seg_next, values_next, c_next, b_next, dt_next, decay, skip)
    return (out_next, grad_values)


def solution(mesh):
    in_specs = (
        P("seq", None), P("seq", "fsdp"), P(), P(("seq", "fsdp"), None), P(("seq", "fsdp"), None),
        P(), P(), P(), P("seq", None), P("seq", "fsdp"), P(), P("seq", "fsdp"),
    )
    out_specs = (P("seq", "fsdp"), P("seq", "fsdp"))
    return jax.shard_map(body, mesh=mesh, in_specs=in_specs, out_specs=out_specs, check_vma=False)
```

profile of v0, /device:TPU:227, one launch (start us, length us, event | category | flops | bytes accessed | tf_op | source)
XLA Modules:
  0.0 243.0 jit_solution(3211714934011919496)
XLA Ops:
  7.2 0.0 all-gather.2.cloned.1.call-start
  7.2 0.8 fusion.1
  8.0 1.1 fusion.2
  9.1 0.8 concatenate.3
  9.9 0.0 all-gather.2.cloned.1.call-update
  9.9 0.0 reduce-scatter.4.cloned.1.call-start
  10.0 0.8 copy.23.dt_ref
  10.8 0.0 copy-start.4
  10.8 0.0 copy-start.5
  10.9 0.0 copy-start
  10.9 0.0 copy-start.2
  10.9 6.5 %copy.22 = bf16[256,8192]{0,1:T(8,128)(2,1)} copy(bf16[256,8192]{1,0:T(8,128)(2,1)} %param.12) | data formatting | bytes 8388608 | tf_op args[0]
  17.4 0.0 copy-done.4
  17.4 0.0 copy-done.5
  17.4 0.1 dynamic-slice_bitcast_fusion
  17.4 0.9 constant_dynamic-slice_fusion
  18.3 1.1 constant_dynamic-slice_fusion.2
  19.4 0.0 copy-done
  19.4 0.0 copy-done.2
  19.4 6.1 %back_pass.1 = bf16[256,1024]{1,0:T(8,128)(2,1)S(1)} custom-call(s32[4]{0:T(128)S(1)} %copy-done.2, bf16[256,1024]{1,0:T(8,128)(2,1)S(1)} %copy-done, bf16[256,128]{1,0:T(8,128)(2,1)S(1)} %get-tuple-element.7.p_ref, bf16[256,128]{1,0:T(8,128)(2,1)S(1)} %get-tuple-element.6.q_ref, f32[256,16]{1,0:T(8,128)S(1)} %copy.23.dt_ref, ...), custom_call_target="tpu_custom_call" | custom-call | flops 40000000000 | bytes 2097152 | tf_op jit(solution)/shard_map/back_pass/pallas_call | solution.py:221
  25.6 0.0 copy-start.6
  25.6 0.0 copy-start.1
  25.6 0.0 copy-start.3
  25.6 50.3 %all-gather.2.cloned.1.call-done = bf16[1024,2176]{1,0:T(8,128)(2,1)} async-done(((bf16[32,2176]{1,0:T(8,128)(2,1)}), bf16[1024,2176]{1,0:T(8,128)(2,1)}) %all-gather.2.cloned.1.call-update) | async-done | bytes 4456464 | tf_op jit(solution)/shard_map/all_gather | solution.py:276
  75.9 5.5 %convolution_bitcast_fusion = f32[2176,256]{1,0:T(8,128)} fusion(bf16[256,1024]{0,1:T(8,128)(2,1)S(1)} %bitcast.12, bf16[1024,2176]{1,0:T(8,128)(2,1)} %all-gather.2.cloned.1.call-done), kind=kOutput, calls=%fused_computation | convolution fusion | flops 1140850688 | bytes 7208960
  81.4 0.0 reduce-scatter.4.cloned.1.call-update
  81.5 0.0 copy-done.6
  81.5 0.1 dynamic_slice.23
  81.5 89.6 %reduce-scatter.4.cloned.1.call-done = f32[272,256]{1,0:T(8,128)} async-done(((f32[2176,256]{1,0:T(8,128)}), f32[272,256]{1,0:T(8,128)}) %reduce-scatter.4.cloned.1.call-update) | async-done | bytes 278544
  171.2 1.1 copy.28
  172.4 0.1 compare_select_fusion.dt_ref
  172.5 0.0 copy-done.1
  172.5 0.0 copy-done.3
  172.5 62.1 %next_pass.1 = bf16[256,1024]{1,0:T(8,128)(2,1)S(1)} custom-call(s32[4]{0:T(128)S(1)} %copy-done.3, bf16[256,1024]{1,0:T(8,128)(2,1)S(1)} %copy-done.1, bf16[256,128]{1,0:T(8,128)(2,1)S(1)} %get-tuple-element.9.p_ref, bf16[256,128]{1,0:T(8,128)(2,1)S(1)} %get-tuple-element.8.q_ref, f32[256,16]{1,0:T(8,128)S(1)} %compare_select_fusion.dt_ref, ...), custom_call_target="tpu_custom_call" | custom-call | flops 40000000000 | bytes 2097152 | tf_op jit(solution)/shard_map/next_pass/pallas_call | solution.py:221
  234.6 0.8 copy.31
  235.4 0.8 copy.32
  (2 shorter events, 0.0 us)
Async XLA Ops:
  7.2 68.7 %all-gather.2.cloned.1.call-start = ((), (), s32[]{:S(2)}) async-start(), calls=%async_computation.1 | async-start | bytes 4595712 | tf_op jit(solution)/shard_map/all_gather | solution.py:276
  9.9 161.2 %reduce-scatter.4.cloned.1.call-start = ((), (), s32[]{:S(2)}) async-start(), calls=%async_computation.2 | async-start | bytes 2506752
  10.8 6.5 %copy-start.4 = (f32[128]{0:T(128)S(1)}, f32[128]{0:T(128)}, u32[]{:S(2)}) copy-start(f32[128]{0:T(128)} %param.19) | copy-start | bytes 1540
  10.8 6.5 %copy-start.5 = (f32[128]{0:T(128)S(1)}, f32[128]{0:T(128)}, u32[]{:S(2)}) copy-start(f32[128]{0:T(128)} %param.18) | copy-start | bytes 1540
  10.9 8.6 %copy-start = (bf16[256,1024]{1,0:T(8,128)(2,1)S(1)}, bf16[256,1024]{1,0:T(8,128)(2,1)}, u32[]{:S(2)}) copy-start(bf16[256,1024]{1,0:T(8,128)(2,1)} %x_ref.2) | copy-start | bytes 1572868
  10.9 8.6 %copy-start.2 = (s32[4]{0:T(128)S(1)}, s32[4]{0:T(128)}, u32[]{:S(2)}) copy-start(s32[4]{0:T(128)} %len_ref.2) | copy-start | bytes 52
  25.6 55.9 %copy-start.6 = (f32[128]{0:T(128)S(1)}, f32[128]{0:T(128)}, u32[]{:S(2)}) copy-start(f32[128]{0:T(128)} %param.17) | copy-start | bytes 1540
  25.6 146.9 %copy-start.1 = (bf16[256,1024]{1,0:T(8,128)(2,1)S(1)}, bf16[256,1024]{1,0:T(8,128)(2,1)}, u32[]{:S(2)}) copy-start(bf16[256,1024]{1,0:T(8,128)(2,1)} %x_ref.3) | copy-start | bytes 1572868
  25.6 146.9 %copy-start.3 = (s32[4]{0:T(128)S(1)}, s32[4]{0:T(128)}, u32[]{:S(2)}) copy-start(s32[4]{0:T(128)} %len_ref.3) | copy-start | bytes 52
Sparse Core Ops, SparseCore 0:
  10.4 65.4 all-gather.1
  81.6 89.5 reduce-scatter.3
where the time goes:
time: 244 us; the launch traced here: 243 us
  waiting for transfers between devices  140 us (57%)
  Pallas kernels  68.2 us (28%)
  local copies, waits for them, and re-layouts  14.9 us (6%)
  between operations  14.2 us (6%)
  matrix products  5.54 us (2%)
    unnamed x3, waiting for transfers between devices  89.7 us
    pallas_call x2, Pallas kernels, scan_pass(): pl.pallas_call(functools.partial(scan_kernel, back, count, nblocks, heads...  68.2 us
    all_gather x1, waiting for transfers between devices, body(): lax.all_gather(jnp.concatenate(pieces, axis=1), 'seq', axis=0, tiled=True)  50.3 us
    unnamed x19, local copies, waits for them, and re-layouts  10 us
    unnamed x1, matrix products  5.54 us
  transfers between devices with their start and end apart: 2, of which 2 were waited for; matrix products, arithmetic and copies ran while one was open for 4% of the time, Pallas kernels for 3%

commit v1 on v0

--- a/solution.py
+++ b/solution.py
@@ -17,26 +17,25 @@
     back, count, nblocks, heads, groups, head_dim,
     len_ref, x_ref, p_ref, q_ref, dt_ref, decay_ref, skip_ref,
     out_ref,
-    cum_s, cum_t, dt_t, fin_s, fout_s, fexp, inside, pre, keep, inbox, outbox, send_sem, recv_sem,
+    cum_s, cum_t, dt_t, fin_s, fout_s, fexp, inside, pre, keep,
+    give, got, got_keep, back_out, back_in,
+    give_sem, got_sem, keep_send, keep_recv, out_sem, in_sem,
 ):
     me = lax.axis_index("seq")
-    place = count - 1 - me if back else me
-    nxt = me - 1 if back else me + 1
-    prv = me + 1 if back else me - 1
     npair = heads * head_dim // LANES
     per = LANES // head_dim
     pair_group = npair // groups
-    first, last = place == 0, place == count - 1
+    share = npair * LANES // count
+    slices = LANES // share
 
     barrier = pltpu.get_barrier_semaphore()
 
-    @pl.when(jnp.logical_not(first))
-    def _():
-        pl.semaphore_signal(barrier, inc=1, device_id={"seq": prv}, device_id_type=MESH)
-
-    @pl.when(jnp.logical_not(last))
-    def _():
-        pl.semaphore_signal(barrier, inc=1, device_id={"seq": nxt}, device_id_type=MESH)
+    def greet(k, _):
+        peer = lax.rem(me + k, count)
+        pl.semaphore_signal(barrier, inc=1, device_id={"seq": peer}, device_id_type=MESH)
+        return 0
+
+    lax.fori_loop(1, count, greet, 0)
 
     bound = []
     total = jnp.int32(0)
@@ -136,8 +135,16 @@
 
         lax.fori_loop(0, nblocks, one, 0)
 
-    def finish(c, state):
+    def finish(c, _):
+        for j in range(slices):
+            src = c * slices + j
+
+            @pl.when(src != me)
+            def _():
+                home(src).wait_recv()
+
         g = c // pair_group
+        state = back_in[pl.ds(c * slices, slices)].reshape(LANES, LANES).astype(jnp.float32)
         cols = pl.ds(pl.multiple_of(c * LANES, LANES), LANES)
         gl = pl.ds(pl.multiple_of(g * LANES, LANES), LANES)
         for step in range(nblocks):
@@ -146,66 +153,70 @@
             entering = (keep[step, c] * state + pre[step, c]).astype(jnp.bfloat16)
             y = jnp.dot(p_ref[rows, gl], entering, preferred_element_type=jnp.float32)
             out_ref[rows, cols] = (inside[c, rows, :] + fexp[c, rows, :] * y).astype(jnp.bfloat16)
-
-    def hop(c):
+        return 0
+
+    def away(peer, slot):
         return pltpu.make_async_remote_copy(
-            src_ref=outbox.at[c], dst_ref=inbox.at[c], send_sem=send_sem.at[c],
-            recv_sem=recv_sem.at[c], device_id={"seq": nxt}, device_id_type=MESH)
-
-    late = place >= 5
-
-    @pl.when(first)
-    def _():
-        inbox[...] = jnp.zeros_like(inbox)
-
-    pl.semaphore_wait(barrier, jnp.where(first, 0, 1) + jnp.where(last, 0, 1))
-
-    def relay(c, _):
-        @pl.when(jnp.logical_not(first))
+            src_ref=give.at[peer], dst_ref=got.at[slot], send_sem=give_sem, recv_sem=got_sem.at[slot],
+            device_id={"seq": peer}, device_id_type=MESH)
+
+    def away_keep(peer, slot):
+        return pltpu.make_async_remote_copy(
+            src_ref=keep.at[nblocks, peer // slices], dst_ref=got_keep.at[slot], send_sem=keep_send,
+            recv_sem=keep_recv, device_id={"seq": peer}, device_id_type=MESH)
+
+    def home_to(peer, slot):
+        return pltpu.make_async_remote_copy(
+            src_ref=back_out.at[peer], dst_ref=back_in.at[slot], send_sem=out_sem, recv_sem=in_sem.at[slot],
+            device_id={"seq": peer}, device_id_type=MESH)
+
+    def home(src):
+        return home_to(src, src)
+
+    for c in range(npair):
+        give[c * slices:(c + 1) * slices] = pre[nblocks, c].astype(jnp.bfloat16).reshape(slices, share, LANES)
+    got[me] = give[me]
+    got_keep[me] = keep[nblocks, me // slices]
+
+    pl.semaphore_wait(barrier, count - 1)
+
+    def send(k, _):
+        peer = lax.rem(me + k, count)
+        away_keep(peer, me).start()
+        away(peer, me).start()
+        return 0
+
+    lax.fori_loop(1, count, send, 0)
+
+    in_block()
+
+    others = pl.ds(0, count - 1)
+    pltpu.make_async_copy(got_keep.at[others], got_keep.at[others], keep_recv).wait()
+
+    def scan(i, state):
+        p = count - 1 - i if back else i
+
+        @pl.when(p != me)
         def _():
-            hop(c).wait_recv()
-
-        state = inbox[c].astype(jnp.float32)
-
-        @pl.when(jnp.logical_not(last))
+            away(p, p).wait_recv()
+
+        @pl.when(p != me)
         def _():
-            outbox[c] = (keep[nblocks, c] * state + pre[nblocks, c]).astype(jnp.bfloat16)
-            hop(c).start()
-
-        @pl.when(late)
+            back_out[p] = state.astype(jnp.bfloat16)
+            home_to(p, me).start()
+
+        @pl.when(p == me)
         def _():
-            finish(c, state)
-
-        return 0
-
-    def phase(ph, _):
-        @pl.when(ph == jnp.where(late, 0, 1))
-        def _():
-            in_block()
-
-        @pl.when(ph == 0)
-        def _():
-            lax.fori_loop(0, npair, relay, 0)
-
-        return 0
-
-    lax.fori_loop(0, 2, phase, 0)
-
-    @pl.when(jnp.logical_not(late))
-    def _():
-        def one(c, _):
-            finish(c, inbox[c].astype(jnp.float32))
-            return 0
-
-        lax.fori_loop(0, npair, one, 0)
-
-    @pl.when(jnp.logical_not(last))
-    def _():
-        def one(c, _):
-            hop(c).wait_send()
-            return 0
-
-        lax.fori_loop(0, npair, one, 0)
+            back_in[p] = state.astype(jnp.bfloat16)
+
+        return got_keep[p] * state + got[p].astype(jnp.float32)
+
+    lax.fori_loop(0, count, scan, jnp.zeros((share, LANES), jnp.float32))
+    lax.fori_loop(0, npair, finish, 0)
+
+    pltpu.make_async_copy(give.at[others], give.at[others], give_sem).wait()
+    pltpu.make_async_copy(got_keep.at[others], got_keep.at[others], keep_send).wait()
+    pltpu.make_async_copy(back_out.at[others], back_out.at[others], out_sem).wait()
 
 
 def scan_pass(back, lengths, x, p_vec, q_vec, dt, decay, skip):
@@ -216,6 +227,7 @@
     nblocks = tokens // SPAN
     npair = width // LANES
     count = lax.axis_size("seq")
+    share = npair * LANES // count
     vm = pl.BlockSpec(memory_space=pltpu.VMEM)
     f32, bf16 = jnp.float32, jnp.bfloat16
     return pl.pallas_call(
@@ -233,10 +245,17 @@
             pltpu.VMEM((npair, tokens, LANES), f32),
             pltpu.VMEM((nblocks + 1, npair, LANES, LANES), f32),
             pltpu.VMEM((nblocks + 1, npair, 1, LANES), f32),
-            pltpu.VMEM((npair, LANES, LANES), bf16),
-            pltpu.VMEM((npair, LANES, LANES), bf16),
-            pltpu.SemaphoreType.DMA((npair,)),
-            pltpu.SemaphoreType.DMA((npair,)),
+            pltpu.VMEM((count, share, LANES), bf16),
+            pltpu.VMEM((count, share, LANES), bf16),
+            pltpu.VMEM((count, 1, LANES), f32),
+            pltpu.VMEM((count, share, LANES), bf16),
+            pltpu.VMEM((count, share, LANES), bf16),
+            pltpu.SemaphoreType.DMA,
+            pltpu.SemaphoreType.DMA((count,)),
+            pltpu.SemaphoreType.DMA,
+            pltpu.SemaphoreType.DMA,
+            pltpu.SemaphoreType.DMA,
+            pltpu.SemaphoreType.DMA((count,)),
         ],
         compiler_params=pltpu.CompilerParams(
             collective_id=1 if back else 0, has_side_effects=True,

time: 244 us -> 209 us (0.86)
  the two profiles are of different devices: /device:TPU:227 before, /device:TPU:1 now
where the time goes in v1:
time: 209 us
  waiting for transfers between devices  113 us (54%)
  Pallas kernels  60.3 us (29%)
  local copies, waits for them, and re-layouts  14.9 us (7%)
  between operations  14.2 us (7%)
  matrix products  5.54 us (3%)
    unnamed x3, waiting for transfers between devices  80.2 us
    pallas_call x2, Pallas kernels, scan_pass(): pl.pallas_call(functools.partial(scan_kernel, back, count, nblocks, heads...  60.3 us
    all_gather x1, waiting for transfers between devices, body(): lax.all_gather(jnp.concatenate(pieces, axis=1), 'seq', axis=0, tiled=True)  33.3 us
    unnamed x19, local copies, waits for them, and re-layouts  10 us
    unnamed x1, matrix products  5.54 us
  transfers between devices with their start and end apart: 2, of which 2 were waited for; matrix products, arithmetic and copies ran while one was open for 5% of the time, Pallas kernels for 17%

profile of v1, /device:TPU:1, one launch (start us, length us, event | category | flops | bytes accessed | tf_op | source)
XLA Modules:
  0.0 208.6 jit_solution(14368193354641091501)
XLA Ops:
  7.2 0.0 all-gather.2.cloned.1.call-start
  7.2 0.8 fusion.1
  8.0 1.1 fusion.2
  9.1 0.8 concatenate.3
  9.9 0.0 all-gather.2.cloned.1.call-update
  9.9 0.0 reduce-scatter.4.cloned.1.call-start
  10.0 0.8 copy.23.dt_ref
  10.8 0.0 copy-start.4
  10.8 0.0 copy-start.5
  10.9 0.0 copy-start
  10.9 0.0 copy-start.2
  10.9 6.5 %copy.22 = bf16[256,8192]{0,1:T(8,128)(2,1)} copy(bf16[256,8192]{1,0:T(8,128)(2,1)} %param.12) | data formatting | bytes 8388608 | tf_op args[0]
  17.4 0.0 copy-done.4
  17.4 0.0 copy-done.5
  17.4 0.1 dynamic-slice_bitcast_fusion
  17.4 0.9 constant_dynamic-slice_fusion
  18.3 1.1 constant_dynamic-slice_fusion.2
  19.4 0.0 copy-done
  19.4 0.0 copy-done.2
  19.4 35.0 %back_pass.1 = bf16[256,1024]{1,0:T(8,128)(2,1)S(1)} custom-call(s32[4]{0:T(128)S(1)} %copy-done.2, bf16[256,1024]{1,0:T(8,128)(2,1)S(1)} %copy-done, bf16[256,128]{1,0:T(8,128)(2,1)S(1)} %get-tuple-element.7.p_ref, bf16[256,128]{1,0:T(8,128)(2,1)S(1)} %get-tuple-element.6.q_ref, f32[256,16]{1,0:T(8,128)S(1)} %copy.23.dt_ref, ...), custom_call_target="tpu_custom_call" | custom-call | flops 40000000000 | bytes 2097152 | tf_op jit(solution)/shard_map/back_pass/pallas_call | solution.py:233
  54.4 0.0 copy-start.6
  54.4 0.0 copy-start.1
  54.5 0.0 copy-start.3
  54.5 33.3 %all-gather.2.cloned.1.call-done = bf16[1024,2176]{1,0:T(8,128)(2,1)} async-done(((bf16[32,2176]{1,0:T(8,128)(2,1)}), bf16[1024,2176]{1,0:T(8,128)(2,1)}) %all-gather.2.cloned.1.call-update) | async-done | bytes 4456464 | tf_op jit(solution)/shard_map/all_gather | solution.py:295
  87.8 5.5 %convolution_bitcast_fusion = f32[2176,256]{1,0:T(8,128)} fusion(bf16[256,1024]{0,1:T(8,128)(2,1)S(1)} %bitcast.12, bf16[1024,2176]{1,0:T(8,128)(2,1)} %all-gather.2.cloned.1.call-done), kind=kOutput, calls=%fused_computation | convolution fusion | flops 1140850688 | bytes 7208960
  93.3 0.0 reduce-scatter.4.cloned.1.call-update
  93.3 0.0 copy-done.6
  93.3 0.1 dynamic_slice.23
  93.4 80.1 %reduce-scatter.4.cloned.1.call-done = f32[272,256]{1,0:T(8,128)} async-done(((f32[2176,256]{1,0:T(8,128)}), f32[272,256]{1,0:T(8,128)}) %reduce-scatter.4.cloned.1.call-update) | async-done | bytes 278544
  173.5 1.1 copy.28
  174.7 0.1 compare_select_fusion.dt_ref
  174.8 0.0 copy-done.1
  174.8 0.0 copy-done.3
  174.8 25.3 %next_pass.1 = bf16[256,1024]{1,0:T(8,128)(2,1)S(1)} custom-call(s32[4]{0:T(128)S(1)} %copy-done.3, bf16[256,1024]{1,0:T(8,128)(2,1)S(1)} %copy-done.1, bf16[256,128]{1,0:T(8,128)(2,1)S(1)} %get-tuple-element.9.p_ref, bf16[256,128]{1,0:T(8,128)(2,1)S(1)} %get-tuple-element.8.q_ref, f32[256,16]{1,0:T(8,128)S(1)} %compare_select_fusion.dt_ref, ...), custom_call_target="tpu_custom_call" | custom-call | flops 40000000000 | bytes 2097152 | tf_op jit(solution)/shard_map/next_pass/pallas_call | solution.py:233
  200.1 0.8 copy.31
  200.9 0.8 copy.32
  (2 shorter events, 0.0 us)
Async XLA Ops:
  7.2 80.6 %all-gather.2.cloned.1.call-start = ((), (), s32[]{:S(2)}) async-start(), calls=%async_computation.1 | async-start | bytes 4595712 | tf_op jit(solution)/shard_map/all_gather | solution.py:295
  9.9 163.6 %reduce-scatter.4.cloned.1.call-start = ((), (), s32[]{:S(2)}) async-start(), calls=%async_computation.2 | async-start | bytes 2506752
  10.8 6.5 %copy-start.4 = (f32[128]{0:T(128)S(1)}, f32[128]{0:T(128)}, u32[]{:S(2)}) copy-start(f32[128]{0:T(128)} %param.19) | copy-start | bytes 1540
  10.8 6.5 %copy-start.5 = (f32[128]{0:T(128)S(1)}, f32[128]{0:T(128)}, u32[]{:S(2)}) copy-start(f32[128]{0:T(128)} %param.18) | copy-start | bytes 1540
  10.9 8.6 %copy-start = (bf16[256,1024]{1,0:T(8,128)(2,1)S(1)}, bf16[256,1024]{1,0:T(8,128)(2,1)}, u32[]{:S(2)}) copy-start(bf16[256,1024]{1,0:T(8,128)(2,1)} %x_ref.2) | copy-start | bytes 1572868
  10.9 8.6 %copy-start.2 = (s32[4]{0:T(128)S(1)}, s32[4]{0:T(128)}, u32[]{:S(2)}) copy-start(s32[4]{0:T(128)} %len_ref.2) | copy-start | bytes 52
  54.4 38.9 %copy-start.6 = (f32[128]{0:T(128)S(1)}, f32[128]{0:T(128)}, u32[]{:S(2)}) copy-start(f32[128]{0:T(128)} %param.17) | copy-start | bytes 1540
  54.4 120.4 %copy-start.1 = (bf16[256,1024]{1,0:T(8,128)(2,1)S(1)}, bf16[256,1024]{1,0:T(8,128)(2,1)}, u32[]{:S(2)}) copy-start(bf16[256,1024]{1,0:T(8,128)(2,1)} %x_ref.3) | copy-start | bytes 1572868
  54.5 120.4 %copy-start.3 = (s32[4]{0:T(128)S(1)}, s32[4]{0:T(128)}, u32[]{:S(2)}) copy-start(s32[4]{0:T(128)} %len_ref.3) | copy-start | bytes 52
Sparse Core Ops, SparseCore 0:
  10.4 77.3 all-gather.1
  93.4 80.0 reduce-scatter.3

commit v2 on v0

v2 whole, which is shorter than its diff:
```python
import functools
import types

import jax
import jax.numpy as jnp
from jax import lax
from jax.experimental import pallas as pl
from jax.experimental.pallas import tpu as pltpu
from jax.sharding import PartitionSpec as P

SPAN = 128
LANES = 128
LEVEL = 4
MESH = pl.DeviceIdType.MESH
F32, BF16 = jnp.float32, jnp.bfloat16


def side_scratch(count, tokens, heads, npair, nblocks, share):
    return dict(
        cum_s=pltpu.VMEM((tokens, heads), F32),
        cum_t=pltpu.VMEM((nblocks, heads, SPAN), F32),
        dt_s=pltpu.VMEM((tokens, heads), F32),
        dt_t=pltpu.VMEM((nblocks, heads, SPAN), F32),
        fin_s=pltpu.VMEM((tokens, heads), F32),
        fout_s=pltpu.VMEM((tokens, heads), F32),
        carry=pltpu.VMEM((nblocks, npair, 1, LANES), F32),
        fexp=pltpu.VMEM((npair, tokens, LANES), F32),
        inside=pltpu.VMEM((npair, tokens, LANES), F32),
        pre=pltpu.VMEM((nblocks + 1, npair, LANES, LANES), F32),
        keep=pltpu.VMEM((nblocks + 1, npair, 1, LANES), F32),
        give=pltpu.VMEM((count, share, LANES), BF16),
        got=pltpu.VMEM((count, share, LANES), BF16),
        got_keep=pltpu.VMEM((count, 1, LANES), F32),
        back_out=pltpu.VMEM((count, share, LANES), BF16),
        back_in=pltpu.VMEM((count, share, LANES), BF16),
        give_sem=pltpu.SemaphoreType.DMA,
        got_sem=pltpu.SemaphoreType.DMA((count,)),
        keep_send=pltpu.SemaphoreType.DMA,
        keep_recv=pltpu.SemaphoreType.DMA,
        out_sem=pltpu.SemaphoreType.DMA,
        in_sem=pltpu.SemaphoreType.DMA((count,)),
    )


class Side:
    def __init__(self, back, me, count, dims, r, len_ref, x_ref, p_ref, q_ref, out_ref, decay_ref, skip_ref):
        self.back, self.me, self.count, self.r = back, me, count, r
        self.nblocks, self.heads, self.head_dim, self.npair = dims
        self.x, self.p, self.q, self.out = x_ref, p_ref, q_ref, out_ref
        self.decay, self.skip = decay_ref, skip_ref
        self.per = LANES // self.head_dim
        self.share = self.npair * LANES // count
        self.slices = LANES // self.share
        self.bound = []
        total = jnp.int32(0)
        for k in range(3):
            total = total + len_ref[k]
            self.bound.append(total)
        self.slab = me * (self.nblocks * SPAN)
        self.dim0 = lax.broadcasted_iota(jnp.int32, (SPAN, SPAN), 0)
        self.dim1 = lax.broadcasted_iota(jnp.int32, (SPAN, SPAN), 1)
        self.lane = lax.broadcasted_iota(jnp.int32, (1, LANES), 1)

    def seg_of(self, pos):
        s = jnp.zeros_like(pos)
        for b in self.bound:
            s = s + (b <= pos).astype(jnp.int32)
        return s

    def widen(self, a, c):
        res = a[:, c * self.per:c * self.per + 1]
        for k in range(1, self.per):
            res = jnp.where(self.lane >= k * self.head_dim, a[:, c * self.per + k:c * self.per + k + 1], res)
        return jnp.broadcast_to(res, (a.shape[0], LANES))

    def order(self):
        for step in range(self.nblocks):
            b = self.nblocks - 1 - step if self.back else step
            yield step, b, slice(b * SPAN, (b + 1) * SPAN)

    def factors(self, dt_of):
        r, heads = self.r, self.heads
        tril = (self.dim0 >= self.dim1).astype(F32)
        for c in range(self.npair):
            r.keep[0, c] = jnp.ones((1, LANES), F32)
        for step, b, rows in self.order():
            dt, dt_t = dt_of(b, rows)
            cum = jnp.dot(tril, -(dt * self.decay[...]), precision=lax.Precision.HIGHEST,
                          preferred_element_type=F32)
            end = cum[SPAN - 1:SPAN, :]
            r.cum_s[rows, :] = cum
            r.cum_t[b] = cum.T
            r.dt_s[rows, :] = dt
            r.dt_t[b] = dt_t
            pos = self.slab + b * SPAN + lax.broadcasted_iota(jnp.int32, (SPAN, heads), 0)
            seg = self.seg_of(pos)
            edge = self.slab + b * SPAN + lax.broadcasted_iota(jnp.int32, (1, heads), 0) * 0
            seg_e = self.seg_of(edge + (SPAN - 1))
            seg_b = jnp.where(edge == 0, 0, self.seg_of(edge - 1))
            send = jnp.where(seg == seg_e, jnp.exp(end - cum), 0.0) * dt
            read = jnp.where(seg == seg_b, jnp.exp(cum), 0.0)
            carry = jnp.where(seg_e == seg_b, jnp.exp(end), 0.0)
            r.fin_s[rows, :] = read if self.back else send
            r.fout_s[rows, :] = send if self.back else read
            for c in range(self.npair):
                wide = self.widen(carry, c)
                r.carry[step, c] = wide
                r.keep[step + 1, c] = wide * r.keep[step, c]
        r.got_keep[self.me] = r.keep[self.nblocks, self.me // self.slices]

    def locals(self):
        r, nblocks = self.r, self.nblocks
        for step, b, rows in self.order():
            qt = self.q[rows, :].T
            f_in = r.fin_s[rows, :]
            for c in range(self.npair):
                cols = slice(c * LANES, (c + 1) * LANES)
                sent = (self.x[rows, cols].astype(F32) * self.widen(f_in, c)).astype(BF16)
                loc = jnp.dot(qt, sent, preferred_element_type=F32)
                if step == 0:
                    r.pre[step, c] = jnp.zeros((LANES, LANES), F32)
                    r.pre[step + 1, c] = loc
                else:
                    r.pre[step + 1, c] = r.carry[step, c] * r.pre[step, c] + loc
        for c in range(self.npair):
            r.give[c * self.slices:(c + 1) * self.slices] = (
                r.pre[nblocks, c].astype(BF16).reshape(self.slices, self.share, LANES))
        r.got[self.me] = r.give[self.me]

    def away(self, peer, slot):
        r = self.r
        return pltpu.make_async_remote_copy(
            src_ref=r.give.at[peer], dst_ref=r.got.at[slot], send_sem=r.give_sem, recv_sem=r.got_sem.at[slot],
            device_id={"seq": peer}, device_id_type=MESH)

    def away_keep(self, peer, slot):
        r = self.r
        return pltpu.make_async_remote_copy(
            src_ref=r.keep.at[self.nblocks, peer // self.slices], dst_ref=r.got_keep.at[slot],
            send_sem=r.keep_send, recv_sem=r.keep_recv, device_id={"seq": peer}, device_id_type=MESH)

    def home(self, peer, slot):
        r = self.r
        return pltpu.make_async_remote_copy(
            src_ref=r.back_out.at[peer], dst_ref=r.back_in.at[slot], send_sem=r.out_sem,
            recv_sem=r.in_sem.at[slot], device_id={"seq": peer}, device_id_type=MESH)

    def send_keeps(self):
        def one(k, _):
            self.away_keep(lax.rem(self.me + k, self.count), self.me).start()
            return 0

        lax.fori_loop(1, self.count, one, 0)

    def send_locals(self):
        def one(k, _):
            self.away(lax.rem(self.me + k, self.count), self.me).start()
            return 0

        lax.fori_loop(1, self.count, one, 0)

    def in_block(self, b):
        r, per, head_dim = self.r, self.per, self.head_dim
        start = b * SPAN
        rows = slice(start, start + SPAN)
        seg_i = self.seg_of(self.slab + start + self.dim0)
        seg_j = self.seg_of(self.slab + start + self.dim1)
        ordered = (self.dim1 >= self.dim0) if self.back else (self.dim1 <= self.dim0)
        bias = jnp.where((seg_i == seg_j) & ordered, 0.0, -jnp.inf)
        cum = r.cum_s[rows, :]
        dt = r.dt_s[rows, :]
        f_out = r.fout_s[rows, :]
        score = lax.dot_general(self.p[rows, :], self.q[rows, :], (((1,), (1,)), ((), ())),
                                preferred_element_type=F32)
        for c in range(self.npair):
            cols = slice(c * LANES, (c + 1) * LANES)
            x = self.x[rows, cols]
            mixes, parts = [], []
            for k in range(per):
                h = c * per + k
                col = cum[:, h:h + 1]
                row = r.cum_t[b, h:h + 1, :]
                spread = (row - col) if self.back else (col - row)
                w = jnp.exp(spread + bias) * score
                if not self.back:
                    w = w * r.dt_t[b, h:h + 1, :]
                mixes.append(w.astype(BF16))
                mine = (self.lane >= k * head_dim) & (self.lane < (k + 1) * head_dim)
                parts.append(jnp.where(mine, x, jnp.zeros_like(x)))
            acc = jnp.dot(jnp.concatenate(mixes, 1), jnp.concatenate(parts, 0), preferred_element_type=F32)
            if self.back:
                acc = acc * self.widen(dt, c)
            r.inside[c, rows, :] = acc + self.widen(self.skip[...], c) * x.astype(F32)
            r.fexp[c, rows, :] = self.widen(f_out, c)

    def scan(self):
        r, me, count = self.r, self.me, self.count
        others = pl.ds(0, count - 1)
        pltpu.make_async_copy(r.got_keep.at[others], r.got_keep.at[others], r.keep_recv).wait()

        def one(i, state):
            p = count - 1 - i if self.back else i

            @pl.when(p != me)
            def _():
                self.away(p, p).wait_recv()
                r.back_out[p] = state.astype(BF16)
                self.home(p, me).start()

            @pl.when(p == me)
            def _():
                r.back_in[p] = state.astype(BF16)

            return r.got_keep[p] * state + r.got[p].astype(F32)

        lax.fori_loop(0, count, one, jnp.zeros((self.share, LANES), F32))

    def finish(self):
        r, me, slices = self.r, self.me, self.slices

        def one(c, _):
            for j in range(slices):
                src = c * slices + j

                @pl.when(src != me)
                def _():
                    self.home(src, src).wait_recv()

            state = r.back_in[pl.ds(c * slices, slices)].reshape(LANES, LANES).astype(F32)
            cols = pl.ds(pl.multiple_of(c * LANES, LANES), LANES)
            for step, b, rows in self.order():
                entering = (r.keep[step, c] * state + r.pre[step, c]).astype(BF16)
                y = jnp.dot(self.p[rows, :], entering, preferred_element_type=F32)
                self.out[rows, cols] = (r.inside[c, rows, :] + r.fexp[c, rows, :] * y).astype(BF16)
            return 0

        lax.fori_loop(0, self.npair, one, 0)

    def drain(self):
        r = self.r
        others = pl.ds(0, self.count - 1)
        pltpu.make_async_copy(r.give.at[others], r.give.at[others], r.give_sem).wait()
        pltpu.make_async_copy(r.got_keep.at[others], r.got_keep.at[others], r.keep_send).wait()
        pltpu.make_async_copy(r.back_out.at[others], r.back_out.at[others], r.out_sem).wait()


def layer_kernel(names, count, nfsdp, dims, *refs):
    r = types.SimpleNamespace(**dict(zip(names, refs)))
    nblocks, heads, head_dim, npair = dims
    me = lax.axis_index("seq")
    fs = lax.axis_index("fsdp")
    part = lax.rem(fs, 2)
    group = fs // 2
    half = r.proj_bc.shape[1] // 2
    rows_dev = r.proj_bc.shape[0]
    tall = nfsdp * rows_dev
    nlevels = count // LEVEL

    barrier = pltpu.get_barrier_semaphore()

    def greet_seq(k, _):
        pl.semaphore_signal(barrier, inc=1, device_id={"seq": lax.rem(me + k, count)}, device_id_type=MESH)
        return 0

    def greet_fsdp(k, _):
        pl.semaphore_signal(barrier, inc=1, device_id={"fsdp": lax.rem(fs + k, nfsdp)}, device_id_type=MESH)
        return 0

    lax.fori_loop(1, nfsdp, greet_fsdp, 0)
    lax.fori_loop(1, count, greet_seq, 0)

    bcol = pl.ds(pl.multiple_of(group * LANES, LANES), LANES)
    ccol = pl.ds(pl.multiple_of(half + group * LANES, LANES), LANES)
    loads = [
        pltpu.make_async_copy(r.grad_hbm, r.grad_v, r.load_sem.at[0]),
        pltpu.make_async_copy(r.bc_prev.at[:, ccol], r.c_prev, r.load_sem.at[1]),
        pltpu.make_async_copy(r.bc_prev.at[:, bcol], r.b_prev, r.load_sem.at[2]),
        pltpu.make_async_copy(r.values_hbm, r.values_v, r.load_sem.at[3]),
        pltpu.make_async_copy(r.hidden_hbm, r.hidden_v, r.load_sem.at[4]),
    ]
    for load in loads:
        load.start()

    def sub(prefix):
        return types.SimpleNamespace(**{k[len(prefix):]: v for k, v in vars(r).items() if k.startswith(prefix)})

    prev = Side(True, me, count, dims, sub("prev_"), r.seg_prev, r.grad_v, r.b_prev, r.c_prev, r.grad_values,
                r.decay, r.skip)
    nxt = Side(False, me, count, dims, sub("next_"), r.seg_next, r.values_v, r.bc_new.at[1], r.bc_new.at[0],
               r.out_next, r.decay, r.skip)

    def dt_prev_of(b, rows):
        dt_t = r.dt_prev_t[:, rows]
        return dt_t.T, dt_t

    prev.factors(dt_prev_of)
    loads[0].wait()
    loads[1].wait()
    prev.locals()

    pl.semaphore_wait(barrier, count + nfsdp - 2)

    def cols_for(peer):
        return pl.ds(pl.multiple_of(lax.rem(peer, 2) * half + (peer // 2) * LANES, LANES), LANES)

    def hand_bc(peer, slot):
        at = pl.ds(pl.multiple_of(slot * rows_dev, rows_dev), rows_dev)
        return pltpu.make_async_remote_copy(
            src_ref=r.proj_bc.at[:, cols_for(peer)], dst_ref=r.weights.at[me, at], send_sem=r.hand_send.at[0],
            recv_sem=r.hand_recv.at[0], device_id={"fsdp": peer}, device_id_type=MESH)

    def hand_dt(peer, slot):
        return pltpu.make_async_remote_copy(
            src_ref=r.proj_dt, dst_ref=r.dt_rows.at[slot], send_sem=r.hand_send.at[1],
            recv_sem=r.hand_recv.at[1], device_id={"fsdp": peer}, device_id_type=MESH)

    def hand(k, _):
        peer = lax.rem(fs + k, nfsdp)
        hand_bc(peer, fs).start()
        hand_dt(peer, fs).start()
        return 0

    lax.fori_loop(1, nfsdp, hand, 0)
    r.weights[me, pl.ds(pl.multiple_of(fs * rows_dev, rows_dev), rows_dev), :] = r.proj_bc[:, cols_for(fs)]
    r.dt_rows[fs] = r.proj_dt[...]

    prev.send_keeps()
    prev.send_locals()
    loads[2].wait()
    prev.in_block(0)

    most = pl.ds(0, (nfsdp - 1) * rows_dev)
    pltpu.make_async_copy(r.weights.at[me, most], r.weights.at[me, most], r.hand_recv.at[0]).wait()
    pltpu.make_async_copy(r.dt_rows.at[pl.ds(0, nfsdp - 1)], r.dt_rows.at[pl.ds(0, nfsdp - 1)],
                          r.hand_recv.at[1]).wait()
    lane = lax.broadcasted_iota(jnp.int32, (rows_dev, LANES), 1)
    packed = jnp.zeros((rows_dev, LANES), F32)
    for g in range(nfsdp):
        turn = lax.rem((g - fs + nfsdp) * heads, LANES)
        moved = pltpu.roll(r.dt_rows[g].astype(F32), turn, 1)
        packed = jnp.where(lane // heads == g, moved, packed)
    r.weights[me, tall:tall + rows_dev, :] = packed.astype(BF16)

    up = lax.rem(me + LEVEL, count)
    down = lax.rem(me + count - LEVEL, count)
    sib = me + 1 - 2 * lax.rem(me, 2)
    other_x = me + 2 - 4 * lax.rem(me // 2, 2)

    def chunk(src, to):
        return pltpu.make_async_remote_copy(
            src_ref=r.weights.at[src], dst_ref=r.weights.at[src], send_sem=r.ring_send,
            recv_sem=r.ring_recv.at[src], device_id={"seq": to}, device_id_type=MESH)

    def at(base, k):
        return lax.rem(base + (count + k * LEVEL), count)

    def relay(src, *targets):
        chunk(src, sib).wait_recv()
        for to in targets:
            chunk(src, to).start()

    for to in (up, down, other_x, sib):
        chunk(me, to).start()

    def level(k, first=False):
        z = lax.rem(me // LEVEL + nlevels + k, nlevels)
        chunk(at(sib, k), sib).wait_recv()
        chunk(at(sib + other_x - me, k), sib).wait_recv()
        lhs = r.hidden_v[:, pl.ds(pl.multiple_of(z * LEVEL * tall, LEVEL * tall), LEVEL * tall)]
        row = lax.broadcasted_iota(jnp.int32, (tall, LANES), 0)
        col = lax.broadcasted_iota(jnp.int32, (tall, LANES), 1)
        own = (row // rows_dev) == (col // heads)
        tiles = []
        for j in range(LEVEL):
            s = z * LEVEL + j
            dt_w = r.weights[s, tall:tall + rows_dev, :]
            spread = jnp.concatenate([dt_w] * nfsdp, 0)
            tiles.append(jnp.concatenate(
                [r.weights[s, 0:tall, :], jnp.where(own, spread, jnp.zeros_like(spread))], 1))
        res = jnp.dot(lhs, jnp.concatenate(tiles, 0), preferred_element_type=F32)
        r.sums[...] = res if first else r.sums[...] + res

    prev.in_block(1)
    relay(at(me, -1), up, other_x, sib)
    relay(at(me, 1), down, other_x, sib)
    relay(other_x, sib)
    prev.scan()
    relay(at(me, -2), up, other_x, sib)
    relay(at(me, 2), down, other_x, sib)
    relay(at(other_x, -1), sib)
    relay(at(other_x, 1), sib)
    loads[4].wait()
    level(0, first=True)
    relay(at(me, -3), up, other_x, sib)
    relay(at(me, 3), other_x, sib)
    relay(at(other_x, -2), sib)
    relay(at(other_x, 2), sib)
    level(-1)
    level(1)
    relay(at(me, -4), other_x, sib)
    relay(at(other_x, -3), sib)
    relay(at(other_x, 3), sib)
    level(-2)
    level(2)
    relay(at(other_x, -4), sib)
    level(-3)
    level(3)
    level(-4)

    mate = fs + 1 - 2 * part
    r.bc_new[part] = r.sums[:, 0:LANES].astype(BF16)
    swap = pltpu.make_async_remote_copy(
        src_ref=r.bc_new.at[part], dst_ref=r.bc_new.at[part], send_sem=r.swap_send, recv_sem=r.swap_recv,
        device_id={"fsdp": mate}, device_id_type=MESH)
    swap.start()

    def dt_next_of(b, rows):
        v = r.sums[rows, LANES:2 * LANES]
        turn = LANES // 2
        while turn >= heads:
            v = v + pltpu.roll(v, turn, 1)
            turn //= 2
        v = v[:, 0:heads] + r.dt_bias[...]
        dt = jnp.maximum(v, 0.0) + jnp.log1p(jnp.exp(-jnp.abs(v)))
        return dt, dt.T

    nxt.factors(dt_next_of)
    nxt.send_keeps()
    loads[3].wait()
    swap.wait_recv()
    nxt.locals()
    nxt.send_locals()
    for b in range(nblocks):
        nxt.in_block(b)
    prev.finish()
    nxt.scan()
    nxt.finish()

    prev.drain()
    nxt.drain()
    swap.wait_send()
    pltpu.make_async_copy(r.weights.at[0, most], r.weights.at[0, most], r.hand_send.at[0]).wait()
    pltpu.make_async_copy(r.dt_rows.at[pl.ds(0, nfsdp - 1)], r.dt_rows.at[pl.ds(0, nfsdp - 1)],
                          r.hand_send.at[1]).wait()
    pltpu.make_async_copy(r.weights.at[pl.ds(0, count - 1)], r.weights.at[pl.ds(0, count - 1)], r.ring_send).wait()


def body(
    hidden_next, values_next, seg_next, proj_bc, proj_dt, dt_bias, decay_rate, skip_gain,
    bc_prev, dt_prev, seg_prev, grad_prev,
):
    tokens, width = values_next.shape
    nfsdp = lax.axis_size("fsdp")
    count = lax.axis_size("seq")
    heads = proj_dt.shape[1] // nfsdp
    head_dim = width // heads
    npair = width // LANES
    nblocks = tokens // SPAN
    share = npair * LANES // count
    rows_dev = proj_bc.shape[0]
    tall = nfsdp * rows_dev
    first_head = lax.axis_index("fsdp") * heads

    def mine(v):
        return lax.dynamic_slice_in_dim(v, first_head, heads, 0)[None]

    vm, sm, hbm = (pl.BlockSpec(memory_space=s) for s in (pltpu.VMEM, pltpu.SMEM, pl.ANY))
    ins = dict(
        seg_next=(seg_next, sm), seg_prev=(seg_prev, sm),
        proj_bc=(proj_bc, vm), proj_dt=(proj_dt, vm),
        dt_bias=(mine(dt_bias), vm), decay=(mine(decay_rate), vm), skip=(mine(skip_gain), vm),
        dt_prev_t=(dt_prev.T, vm),
        hidden_hbm=(hidden_next, hbm), values_hbm=(values_next, hbm), grad_hbm=(grad_prev, hbm),
        bc_prev=(bc_prev, hbm),
    )
    scratch = dict(
        grad_v=pltpu.VMEM((tokens, width), BF16),
        values_v=pltpu.VMEM((tokens, width), BF16),
        hidden_v=pltpu.VMEM(hidden_next.shape, BF16),
        b_prev=pltpu.VMEM((tokens, LANES), BF16),
        c_prev=pltpu.VMEM((tokens, LANES), BF16),
        weights=pltpu.VMEM((count, tall + rows_dev, LANES), BF16),
        dt_rows=pltpu.VMEM((nfsdp, rows_dev, LANES), BF16),
        sums=pltpu.VMEM((tokens, 2 * LANES), F32),
        bc_new=pltpu.VMEM((2, tokens, LANES), BF16),
        load_sem=pltpu.SemaphoreType.DMA((5,)),
        hand_send=pltpu.SemaphoreType.DMA((2,)),
        hand_recv=pltpu.SemaphoreType.DMA((2,)),
        ring_send=pltpu.SemaphoreType.DMA,
        ring_recv=pltpu.SemaphoreType.DMA((count,)),
        swap_send=pltpu.SemaphoreType.DMA,
        swap_recv=pltpu.SemaphoreType.DMA,
    )
    for name in ("prev", "next"):
        for key, val in side_scratch(count, tokens, heads, npair, nblocks, share).items():
            scratch[f"{name}_{key}"] = val
    names = list(ins) + ["out_next", "grad_values"] + list(scratch)
    out = jax.ShapeDtypeStruct((tokens, width), BF16)
    return pl.pallas_call(
        functools.partial(layer_kernel, names, count, nfsdp, (nblocks, heads, head_dim, npair)),
        out_shape=(out, out),
        in_specs=[spec for _, spec in ins.values()],
        out_specs=(vm, vm),
        scratch_shapes=list(scratch.values()),
        compiler_params=pltpu.CompilerParams(
            collective_id=0, has_side_effects=True, vmem_limit_bytes=60 * 1024 * 1024),
        cost_estimate=pl.CostEstimate(flops=4_000_000_000, bytes_accessed=16 * tokens * width, transcendentals=0),
        name="layer",
    )(*[val for val, _ in ins.values()])


def solution(mesh):
    in_specs = (
        P("seq", None), P("seq", "fsdp"), P(), P(("seq", "fsdp"), None), P(("seq", "fsdp"), None),
        P(), P(), P(), P("seq", None), P("seq", "fsdp"), P(), P("seq", "fsdp"),
    )
    out_specs = (P("seq", "fsdp"), P("seq", "fsdp"))
    return jax.shard_map(body, mesh=mesh, in_specs=in_specs, out_specs=out_specs, check_vma=False)
```

time: 244 us -> 69.3 us (0.28)
  the two profiles are of different devices: /device:TPU:227 before, /device:TPU:9 now
where the time goes in v2:
time: 69.3 us; the launch traced here: 69 us
  Pallas kernels  62.1 us (90%)
  local copies, waits for them, and re-layouts  6.29 us (9%)
    pallas_call x1, Pallas kernels, body(): pl.pallas_call(functools.partial(layer_kernel, names, count, nfsdp, (nblo...  62.1 us
    unnamed x4, local copies, waits for them, and re-layouts  4.39 us
    broadcast_in_dim x2, local copies, waits for them, and re-layouts, mine(): return lax.dynamic_slice_in_dim(v, first_head, heads, 0)[None]  1.9 us

profile of v2, /device:TPU:9, one launch (start us, length us, event | category | flops | bytes accessed | tf_op | source)
XLA Modules:
  0.0 69.0 jit_solution(6541174341246287216)
XLA Ops:
  0.6 0.0 copy-start
  0.6 0.6 copy-done
  1.3 0.6 dynamic-slice_bitcast_fusion.2.refs_4_
  1.9 1.3 %dynamic-slice_bitcast_fusion = (f32[1,16]{1,0:T(1,128)}, f32[1,16]{1,0:T(1,128)}) fusion(f32[128]{0:T(128)} %param.19, s32[]{:T(128)S(6)} %select_n.2, f32[128]{0:T(128)} %param.18), kind=kLoop, calls=%fused_computation | loop fusion | bytes 260 | tf_op jit(solution)/shard_map/broadcast_in_dim | solution.py:465
  3.2 62.1 %layer.1 = (bf16[256,1024]{1,0:T(8,128)(2,1)}, bf16[256,1024]{1,0:T(8,128)(2,1)}) custom-call(s32[4]{0:T(128)} %refs_0_.1, s32[4]{0:T(128)} %refs_1_.1, bf16[32,1024]{1,0:T(8,128)(2,1)} %refs_2_.1, bf16[32,128]{1,0:T(8,128)(2,1)} %refs_3_.1, f32[1,16]{1,0:T(1,128)} %dynamic-slice_bitcast_fusion.2.refs_4_, f32[1,16]{1,0:T(1,128)} %get-tuple-element.3.refs_5_, ...), custom_call_target="tpu_custom_call" | custom-call | flops 4000000000 | bytes 4194304 | tf_op jit(solution)/shard_map/layer/pallas_call | solution.py:499
  65.3 1.9 %copy.16 = bf16[256,1024]{1,0:T(8,128)(2,1)} copy(bf16[256,1024]{1,0:T(8,128)(2,1)} %get-tuple-element.6) | data formatting | bytes 1048576
  67.2 1.9 %copy.17 = bf16[256,1024]{1,0:T(8,128)(2,1)} copy(bf16[256,1024]{1,0:T(8,128)(2,1)} %get-tuple-element.7) | data formatting | bytes 1048576
Async XLA Ops:
  0.6 0.7 copy-start

commit v3 on v2

--- a/solution.py
+++ b/solution.py
@@ -266,37 +266,49 @@
         pl.semaphore_signal(barrier, inc=1, device_id={"fsdp": lax.rem(fs + k, nfsdp)}, device_id_type=MESH)
         return 0
 
+    first = [
+        pltpu.make_async_copy(r.proj_bc_hbm, r.proj_bc, r.load_sem.at[0]),
+        pltpu.make_async_copy(r.proj_dt_hbm, r.proj_dt, r.load_sem.at[1]),
+    ]
+    lengths = [
+        pltpu.make_async_copy(r.seg_prev_hbm, r.seg_prev, r.load_sem.at[11]),
+        pltpu.make_async_copy(r.seg_next_hbm, r.seg_next, r.load_sem.at[12]),
+    ]
+    for load in first + lengths:
+        load.start()
     lax.fori_loop(1, nfsdp, greet_fsdp, 0)
     lax.fori_loop(1, count, greet_seq, 0)
 
     bcol = pl.ds(pl.multiple_of(group * LANES, LANES), LANES)
     ccol = pl.ds(pl.multiple_of(half + group * LANES, LANES), LANES)
     loads = [
-        pltpu.make_async_copy(r.grad_hbm, r.grad_v, r.load_sem.at[0]),
-        pltpu.make_async_copy(r.bc_prev.at[:, ccol], r.c_prev, r.load_sem.at[1]),
-        pltpu.make_async_copy(r.bc_prev.at[:, bcol], r.b_prev, r.load_sem.at[2]),
-        pltpu.make_async_copy(r.values_hbm, r.values_v, r.load_sem.at[3]),
-        pltpu.make_async_copy(r.hidden_hbm, r.hidden_v, r.load_sem.at[4]),
+        pltpu.make_async_copy(r.dt_prev_hbm, r.dt_prev_t, r.load_sem.at[2]),
+        pltpu.make_async_copy(r.decay_hbm, r.heads_v.at[0], r.load_sem.at[3]),
+        pltpu.make_async_copy(r.skip_hbm, r.heads_v.at[1], r.load_sem.at[4]),
+        pltpu.make_async_copy(r.bias_hbm, r.heads_v.at[2], r.load_sem.at[5]),
+        pltpu.make_async_copy(r.grad_hbm, r.grad_v, r.load_sem.at[6]),
+        pltpu.make_async_copy(r.bc_prev.at[:, ccol], r.c_prev, r.load_sem.at[7]),
+        pltpu.make_async_copy(r.bc_prev.at[:, bcol], r.b_prev, r.load_sem.at[8]),
+        pltpu.make_async_copy(r.values_hbm, r.values_v, r.load_sem.at[9]),
+        pltpu.make_async_copy(r.hidden_hbm, r.hidden_v, r.load_sem.at[10]),
     ]
     for load in loads:
         load.start()
 
+    for load in lengths:
+        load.wait()
+
     def sub(prefix):
         return types.SimpleNamespace(**{k[len(prefix):]: v for k, v in vars(r).items() if k.startswith(prefix)})
 
     prev = Side(True, me, count, dims, sub("prev_"), r.seg_prev, r.grad_v, r.b_prev, r.c_prev, r.grad_values,
-                r.decay, r.skip)
+                r.mine_v.at[0], r.mine_v.at[1])
     nxt = Side(False, me, count, dims, sub("next_"), r.seg_next, r.values_v, r.bc_new.at[1], r.bc_new.at[0],
-               r.out_next, r.decay, r.skip)
+               r.out_next, r.mine_v.at[0], r.mine_v.at[1])
 
     def dt_prev_of(b, rows):
         dt_t = r.dt_prev_t[:, rows]
         return dt_t.T, dt_t
-
-    prev.factors(dt_prev_of)
-    loads[0].wait()
-    loads[1].wait()
-    prev.locals()
 
     pl.semaphore_wait(barrier, count + nfsdp - 2)
 
@@ -320,13 +332,24 @@
         hand_dt(peer, fs).start()
         return 0
 
+    for load in first:
+        load.wait()
     lax.fori_loop(1, nfsdp, hand, 0)
     r.weights[me, pl.ds(pl.multiple_of(fs * rows_dev, rows_dev), rows_dev), :] = r.proj_bc[:, cols_for(fs)]
     r.dt_rows[fs] = r.proj_dt[...]
 
+    for load in loads[:4]:
+        load.wait()
+    for k in range(3):
+        turned = pltpu.roll(jnp.broadcast_to(r.heads_v[k], (8, LANES)), lax.rem(LANES - fs * heads, LANES), 1)
+        r.mine_v[k] = turned[0:1, 0:heads]
+    prev.factors(dt_prev_of)
     prev.send_keeps()
+    loads[4].wait()
+    loads[5].wait()
+    prev.locals()
     prev.send_locals()
-    loads[2].wait()
+    loads[6].wait()
     prev.in_block(0)
 
     most = pl.ds(0, (nfsdp - 1) * rows_dev)
@@ -384,12 +407,11 @@
     relay(at(me, -1), up, other_x, sib)
     relay(at(me, 1), down, other_x, sib)
     relay(other_x, sib)
-    prev.scan()
     relay(at(me, -2), up, other_x, sib)
     relay(at(me, 2), down, other_x, sib)
     relay(at(other_x, -1), sib)
     relay(at(other_x, 1), sib)
-    loads[4].wait()
+    loads[8].wait()
     level(0, first=True)
     relay(at(me, -3), up, other_x, sib)
     relay(at(me, 3), other_x, sib)
@@ -403,6 +425,7 @@
     level(-2)
     level(2)
     relay(at(other_x, -4), sib)
+    prev.scan()
     level(-3)
     level(3)
     level(-4)
@@ -420,13 +443,13 @@
         while turn >= heads:
             v = v + pltpu.roll(v, turn, 1)
             turn //= 2
-        v = v[:, 0:heads] + r.dt_bias[...]
+        v = v[:, 0:heads] + r.mine_v[2]
         dt = jnp.maximum(v, 0.0) + jnp.log1p(jnp.exp(-jnp.abs(v)))
         return dt, dt.T
 
     nxt.factors(dt_next_of)
     nxt.send_keeps()
-    loads[3].wait()
+    loads[7].wait()
     swap.wait_recv()
     nxt.locals()
     nxt.send_locals()
@@ -459,17 +482,12 @@
     share = npair * LANES // count
     rows_dev = proj_bc.shape[0]
     tall = nfsdp * rows_dev
-    first_head = lax.axis_index("fsdp") * heads
-
-    def mine(v):
-        return lax.dynamic_slice_in_dim(v, first_head, heads, 0)[None]
-
-    vm, sm, hbm = (pl.BlockSpec(memory_space=s) for s in (pltpu.VMEM, pltpu.SMEM, pl.ANY))
+
+    hbm, vm = (pl.BlockSpec(memory_space=m) for m in (pltpu.HBM, pltpu.VMEM))
     ins = dict(
-        seg_next=(seg_next, sm), seg_prev=(seg_prev, sm),
-        proj_bc=(proj_bc, vm), proj_dt=(proj_dt, vm),
-        dt_bias=(mine(dt_bias), vm), decay=(mine(decay_rate), vm), skip=(mine(skip_gain), vm),
-        dt_prev_t=(dt_prev.T, vm),
+        seg_next_hbm=(seg_next, hbm), seg_prev_hbm=(seg_prev, hbm),
+        proj_bc_hbm=(proj_bc, hbm), proj_dt_hbm=(proj_dt, hbm), dt_prev_hbm=(dt_prev.T, hbm),
+        decay_hbm=(decay_rate[None], hbm), skip_hbm=(skip_gain[None], hbm), bias_hbm=(dt_bias[None], hbm),
         hidden_hbm=(hidden_next, hbm), values_hbm=(values_next, hbm), grad_hbm=(grad_prev, hbm),
         bc_prev=(bc_prev, hbm),
     )
@@ -483,7 +501,14 @@
         dt_rows=pltpu.VMEM((nfsdp, rows_dev, LANES), BF16),
         sums=pltpu.VMEM((tokens, 2 * LANES), F32),
         bc_new=pltpu.VMEM((2, tokens, LANES), BF16),
-        load_sem=pltpu.SemaphoreType.DMA((5,)),
+        proj_bc=pltpu.VMEM(proj_bc.shape, BF16),
+        proj_dt=pltpu.VMEM(proj_dt.shape, BF16),
+        dt_prev_t=pltpu.VMEM((heads, tokens), F32),
+        heads_v=pltpu.VMEM((3, 1, LANES), F32),
+        mine_v=pltpu.VMEM((3, 1, heads), F32),
+        seg_next=pltpu.SMEM((4,), jnp.int32),
+        seg_prev=pltpu.SMEM((4,), jnp.int32),
+        load_sem=pltpu.SemaphoreType.DMA((13,)),
         hand_send=pltpu.SemaphoreType.DMA((2,)),
         hand_recv=pltpu.SemaphoreType.DMA((2,)),
         ring_send=pltpu.SemaphoreType.DMA,
@@ -503,10 +528,10 @@
         out_specs=(vm, vm),
         scratch_shapes=list(scratch.values()),
         compiler_params=pltpu.CompilerParams(
-            collective_id=0, has_side_effects=True, vmem_limit_bytes=60 * 1024 * 1024),
+            collective_id=0, has_side_effects=True, vmem_limit_bytes=32 * 1024 * 1024),
         cost_estimate=pl.CostEstimate(flops=4_000_000_000, bytes_accessed=16 * tokens * width, transcendentals=0),
         name="layer",
-    )(*[val for val, _ in ins.values()])
+    )(*[pltpu.with_memory_space_constraint(val, pltpu.HBM) if spec is hbm else val for val, spec in ins.values()])
 
 
 def solution(mesh):

time: 69.3 us -> 61.1 us (0.88)
  the two profiles are of different devices: /device:TPU:9 before, /device:TPU:1 now
where the time goes in v3:
time: 61.1 us; the launch traced here: 59.9 us
  Pallas kernels  57.7 us (94%)
  local copies, waits for them, and re-layouts  1.59 us (3%)
  between operations  0.64 us (1%)
    pallas_call x1, Pallas kernels, body(): pl.pallas_call(functools.partial(layer_kernel, names, count, nfsdp, (nblo...  57.7 us
    unnamed x2, local copies, waits for them, and re-layouts  1.59 us

profile of v3, /device:TPU:1, one launch (start us, length us, event | category | flops | bytes accessed | tf_op | source)
XLA Modules:
  0.0 59.9 jit_solution(16851417521799230550)
XLA Ops:
  0.6 57.7 %layer.1 = (bf16[256,1024]{1,0:T(8,128)(2,1)S(1)}, bf16[256,1024]{1,0:T(8,128)(2,1)S(1)}) custom-call(s32[4]{0:T(128)} %refs_0_.1, s32[4]{0:T(128)} %refs_1_.1, bf16[32,1024]{1,0:T(8,128)(2,1)} %refs_2_.1, bf16[32,128]{1,0:T(8,128)(2,1)} %refs_3_.1, f32[16,256]{1,0:T(8,128)} %bitcast.4, f32[1,128]{1,0:T(1,128)} %bitcast.5, f32[1,128]{1,0:T(1,128)} %bitcast.6, ...), custom_call_target="tpu_custom_call" | custom-call | flops 4000000000 | bytes 4194304 | tf_op jit(solution)/shard_map/layer/pallas_call | solution.py:524
  58.3 0.8 %copy.16 = bf16[256,1024]{1,0:T(8,128)(2,1)} copy(bf16[256,1024]{1,0:T(8,128)(2,1)S(1)} %get-tuple-element.4) | data formatting | bytes 1048576
  59.1 0.8 %copy.17 = bf16[256,1024]{1,0:T(8,128)(2,1)} copy(bf16[256,1024]{1,0:T(8,128)(2,1)S(1)} %get-tuple-element.5) | data formatting | bytes 1048576
